TPU v7x, 16 devices: a whole 2x2x2 slice. The times are simulated.
16 devices in a mesh: col: 2 (over z), row: 8 (over y, x, core).
Axes of the slice: x: 2, y: 2, z: 2, core: 2. Of those that a mesh axis runs over, the one named last changes fastest.
Arguments:
- vel_u: float32 [31, 512, 512], P(None, 'row', 'col')
- vel_v: float32 [31, 512, 512], P(None, 'row', 'col')
- temperature: float32 [31, 512, 512], P(None, 'row', 'col')
- salinity: float32 [31, 512, 512], P(None, 'row', 'col')
- tracers: float32 [31, 10, 512, 512], P(None, None, 'row', 'col')
- surf_eta: float32 [512, 512], P('row', 'col')
- trans_u: float32 [512, 512], P('row', 'col')
- trans_v: float32 [512, 512], P('row', 'col')
- bottom_depth: float32 [512, 512], P('row', 'col')
- level_count: int32 [512, 512], P('row', 'col')
- avg_weights: float32 [30], replicated
Outputs:
- output 1: float32 [512, 512], P('row', 'col')
- output 2: float32 [512, 512], P('row', 'col')
- output 3: float32 [512, 512], P('row', 'col')
- output 4: float32 [31, 512, 512], P(None, 'row', 'col')
- output 5: float32 [31, 512, 512], P(None, 'row', 'col')
- output 6: float32 [31, 512, 512], P(None, 'row', 'col')
- output 7: float32 [31, 512, 512], P(None, 'row', 'col')
- output 8: float32 [31, 10, 512, 512], P(None, None, 'row', 'col')
All inputs are finite; a program needn't handle non-finite values.
Results may differ from a plain program's by a relative error of at most 0.001.
Values sent between devices are 32-bit elements.
A program may use at most 1 GiB of HBM per device.

v0:
```python
import jax
import jax.numpy as jnp
from jax import lax
from jax.sharding import PartitionSpec as P

GRAV_ACC = 400.0
DT_STEP = 0.4
THERMAL_EXP = 0.002
HALINE_CON = 0.004
R_VISC = 2.0
R_DIFF = 0.5


def tridiag_coeffs(active, r_coef, num_lev):
    level_idx = jnp.arange(num_lev)[:, None, None]
    sub_diag = jnp.where((level_idx >= 1) & (level_idx < active[None]), -r_coef, 0.0)
    sup_diag = jnp.where(level_idx + 1 < active[None], -r_coef, 0.0)
    return sub_diag, 1.0 - sub_diag - sup_diag, sup_diag


def tridiag_factor(sub_diag, main_diag, sup_diag):
    def value_a9(c_prev, coef_k):
        sub_k, main_k, sup_k = coef_k
        pivot_k = main_k - sub_k * c_prev
        c_new = sup_k / pivot_k
        return c_new, (c_new, pivot_k)
    c_last, factors = lax.scan(value_a9, jnp.zeros_like(main_diag[0]), (sub_diag, main_diag, sup_diag))
    return factors


def tridiag_apply(sub_diag, c_all, pivots, rhs_all):
    def fwd_step(d_prev, xs_k):
        sub_k, pivot_k, rhs_k = xs_k
        d_new = (rhs_k - sub_k * d_prev) / pivot_k
        return d_new, d_new
    d_last, d_all = lax.scan(fwd_step, jnp.zeros_like(rhs_all[0]), (sub_diag, pivots, rhs_all))
    def back_step(x_next, xs_k):
        c_k, d_k = xs_k
        x_new = d_k - c_k * x_next
        return x_new, x_new
    x_first, x_all = lax.scan(back_step, jnp.zeros_like(rhs_all[0]), (c_all, d_all), reverse=True)
    return x_all


def solution(mesh):
    num_col = mesh.shape["col"]
    num_row = mesh.shape["row"]
    to_west = [(src_dev, (src_dev - 1) % num_col) for src_dev in range(num_col)]
    to_east = [(src_dev, (src_dev + 1) % num_col) for src_dev in range(num_col)]
    to_south = [(src_dev, src_dev - 1) for src_dev in range(1, num_row)]
    to_north = [(src_dev, src_dev + 1) for src_dev in range(num_row - 1)]

    def shift_east(grid_field):
        edge_strip = lax.ppermute(grid_field[..., :1], "col", to_west)
        return jnp.concatenate([grid_field[..., 1:], edge_strip], axis=-1)

    def shift_west(grid_field):
        edge_strip = lax.ppermute(grid_field[..., -1:], "col", to_east)
        return jnp.concatenate([edge_strip, grid_field[..., :-1]], axis=-1)

    def shift_north(grid_field):
        edge_strip = lax.ppermute(grid_field[..., :1, :], "row", to_south)
        return jnp.concatenate([grid_field[..., 1:, :], edge_strip], axis=-2)

    def shift_south(grid_field):
        edge_strip = lax.ppermute(grid_field[..., -1:, :], "row", to_north)
        return jnp.concatenate([edge_strip, grid_field[..., :-1, :]], axis=-2)

    def advect_tracer(tracer_field, u_face, v_face):
        flux_x = u_face * jnp.where(u_face > 0, tracer_field, shift_east(tracer_field))
        flux_y = v_face * jnp.where(v_face > 0, tracer_field, shift_north(tracer_field))
        return tracer_field - DT_STEP * ((flux_x - shift_west(flux_x)) + (flux_y - shift_south(flux_y)))

    def local_step(vel_u, vel_v, value_a11, salinity, tracers, surf_eta, trans_u, trans_v, bottom_depth, level_count, avg_weights):
        num_lev = vel_u.shape[0]
        num_sub = avg_weights.shape[0]
        dt_fast = DT_STEP / num_sub
        level_idx = jnp.arange(num_lev)[:, None, None]
        thick_c = jnp.where(level_count > 0, bottom_depth / jnp.maximum(level_count, 1).astype(jnp.float32), 0.0)
        count_u = jnp.minimum(level_count, shift_east(level_count))
        count_v = jnp.minimum(level_count, shift_north(level_count))
        thick_u = jnp.minimum(thick_c, shift_east(thick_c))
        thick_v = jnp.minimum(thick_c, shift_north(thick_c))
        depth_u = count_u.astype(jnp.float32) * thick_u
        depth_v = count_v.astype(jnp.float32) * thick_v
        mask_c = (level_idx < level_count[None]).astype(jnp.float32)
        mask_u = (level_idx < count_u[None]).astype(jnp.float32)
        mask_v = (level_idx < count_v[None]).astype(jnp.float32)
        wet_c = (level_count > 0).astype(jnp.float32)
        wet_u = (count_u > 0).astype(jnp.float32)
        wet_v = (count_v > 0).astype(jnp.float32)
        u_face = vel_u * mask_u
        v_face = vel_v * mask_v

        density = -THERMAL_EXP * value_a11 + HALINE_CON * salinity
        pressure = GRAV_ACC * thick_c[None] * (jnp.cumsum(density, axis=0) - 0.5 * density)
        u_east = shift_east(u_face)
        u_west = shift_west(u_face)
        u_north = shift_north(u_face)
        u_south = shift_south(u_face)
        v_east = shift_east(v_face)
        v_west = shift_west(v_face)
        v_north = shift_north(v_face)
        v_south = shift_south(v_face)
        v_at_u = 0.25 * (v_face + v_east + v_south + shift_south(v_east))
        u_at_v = 0.25 * (u_face + u_west + u_north + shift_north(u_west))
        tend_u = (-u_face * 0.5 * (u_east - u_west) - v_at_u * 0.5 * (u_north - u_south) - (shift_east(pressure) - pressure)) * mask_u
        tend_v = (-u_at_v * 0.5 * (v_east - v_west) - v_face * 0.5 * (v_north - v_south) - (shift_north(pressure) - pressure)) * mask_v
        force_u = thick_u * jnp.sum(tend_u, axis=0)
        force_v = thick_v * jnp.sum(tend_v, axis=0)
        sub_u, main_u, sup_u = tridiag_coeffs(count_u, R_VISC, num_lev)
        c_u, pivot_u = tridiag_factor(sub_u, main_u, sup_u)
        pred_u = tridiag_apply(sub_u, c_u, pivot_u, u_face + DT_STEP * tend_u)
        sub_v, main_v, sup_v = tridiag_coeffs(count_v, R_VISC, num_lev)
        c_v, pivot_v = tridiag_factor(sub_v, main_v, sup_v)
        pred_v = tridiag_apply(sub_v, c_v, pivot_v, v_face + DT_STEP * tend_v)

        sub_c, main_c, sup_c = tridiag_coeffs(level_count, R_DIFF, num_lev)
        c_c, pivot_c = tridiag_factor(sub_c, main_c, sup_c)
        temp_next = tridiag_apply(sub_c, c_c, pivot_c, advect_tracer(value_a11, u_face, v_face) * mask_c) * mask_c
        salt_next = tridiag_apply(sub_c, c_c, pivot_c, advect_tracer(salinity, u_face, v_face) * mask_c) * mask_c
        mask_t = mask_c[:, None]
        tracers_next = tridiag_apply(sub_c, c_c, pivot_c, advect_tracer(tracers, u_face[:, None], v_face[:, None]) * mask_t) * mask_t

        def subcycle(step_idx, state_bt):
            eta_c, tu_c, tv_c, avg_u, avg_v = state_bt
            weight = avg_weights[step_idx]
            eta_c = (eta_c - dt_fast * ((tu_c - shift_west(tu_c)) + (tv_c - shift_south(tv_c)))) * wet_c
            tu_c = (tu_c + dt_fast * (force_u - GRAV_ACC * depth_u * (shift_east(eta_c) - eta_c))) * wet_u
            tv_c = (tv_c + dt_fast * (force_v - GRAV_ACC * depth_v * (shift_north(eta_c) - eta_c))) * wet_v
            return (eta_c, tu_c, tv_c, avg_u + weight * tu_c, avg_v + weight * tv_c)

        state_init = (surf_eta * wet_c, trans_u * wet_u, trans_v * wet_v, jnp.zeros_like(trans_u), jnp.zeros_like(trans_v))
        eta_next, tu_next, tv_next, avg_u, avg_v = lax.fori_loop(0, num_sub, subcycle, state_init)

        safe_u = jnp.where(count_u > 0, depth_u, 1.0)
        safe_v = jnp.where(count_v > 0, depth_v, 1.0)
        levels_u = jnp.maximum(count_u, 1).astype(jnp.float32)
        levels_v = jnp.maximum(count_v, 1).astype(jnp.float32)
        vel_u_next = (pred_u - (jnp.sum(pred_u, axis=0) / levels_u)[None] + (avg_u / safe_u)[None]) * mask_u
        vel_v_next = (pred_v - (jnp.sum(pred_v, axis=0) / levels_v)[None] + (avg_v / safe_v)[None]) * mask_v
        return eta_next, tu_next, tv_next, vel_u_next, vel_v_next, temp_next, salt_next, tracers_next

    spec_3d = P(None, "row", "col")
    spec_4d = P(None, None, "row", "col")
    spec_2d = P("row", "col")
    in_specs = (spec_3d, spec_3d, spec_3d, spec_3d, spec_4d, spec_2d, spec_2d, spec_2d, spec_2d, spec_2d, P())
    out_specs = (spec_2d, spec_2d, spec_2d, spec_3d, spec_3d, spec_3d, spec_3d, spec_4d)
    return jax.shard_map(local_step, mesh=mesh, in_specs=in_specs, out_specs=out_specs, check_vma=False)
```

profile of v0, /device:TPU:3, one launch (start us, length us, event | category | flops | bytes accessed | tf_op | source)
XLA Modules:
  0.0 1916.4 jit_solution(13756365350814676311)
XLA Ops:
  10.5 37.8 %copy.128 = f32[31,10,64,256]{2,0,3,1:T(8,128)} copy(f32[31,10,64,256]{3,2,1,0:T(8,128)} %param.43) | data formatting | bytes 40632320 | tf_op args[4]
  48.4 31.5 %slice.336 = f32[31,10,63,256]{2,0,3,1:T(8,128)} slice(f32[31,10,64,256]{2,0,3,1:T(8,128)} %copy.128), slice={[0:31], [0:10], [1:64], [0:256]} | slice | bytes 39997440 | tf_op jit(solution)/shard_map/slice | solution.py:63
  79.9 28.9 %slice.332 = f32[31,10,64,255]{2,0,3,1:T(8,128)} slice(f32[31,10,64,256]{2,0,3,1:T(8,128)} %copy.128), slice={[0:31], [0:10], [0:64], [1:256]} | slice | bytes 40473600 | tf_op jit(solution)/shard_map/slice | solution.py:55
  276.2 23.3 %multiply_add_fusion = (f32[31,64,256]{2,1,0:T(8,128)}, f32[31,64,256]{2,1,0:T(8,128)}) fusion(f32[31,64,256]{2,1,0:T(8,128)S(1)} %get-tuple-element.1616, f32[31,64,256]{2,1,0:T(8,128)} %copy-done.7, f32[31,1,256]{2,1,0:T(1,128)} %collective-permute-done.19, f32[31,63,256]{2,1,0:T(8,128)} %slice.322, f32[31,63,256]{2,1,0:T(8,128)} %get-tuple-element.1649, ...), kind=kLoop, calls=%fused_computation.144 | loop fusion | flops 13205504 | bytes 26476544 | tf_op jit(solution)/shard_map/add | solution.py:116
  320.8 14.0 subtract_subtract_fusion
  336.5 48.0 %while.224 = (s32[]{:T(128)}, f32[64,256]{1,0:T(8,128)S(1)}, f32[31,64,256]{2,1,0:T(8,128)S(1)}, f32[31,64,256]{2,1,0:T(8,128)}, f32[31,64,256]{2,1,0:T(8,128)},...) while((s32[]{:T(128)}, f32[64,256]{1,0:T(8,128)S(1)}, ...), condition=%wide.region_20.21_spmd.clone, body=%wide.region_19.20_spmd.clone.sunk | while | flops 65539 | bytes 459367 | solution.py:27
  386.5 48.3 %while.225 = (s32[]{:T(128)}, f32[64,256]{1,0:T(8,128)S(1)}, f32[31,64,256]{2,1,0:T(8,128)}, f32[31,64,256]{2,1,0:T(8,128)}, f32[31,64,256]{2,1,0:T(8,128)}, /*index=5*/f32[31,64,256]{2,1,0:T(8,128)}, s32[]{:T(128)}, s32[]{:T(128)}) while((s32[]{:T(128)}, f32[64,256]{1,0:T(8,128)S(1)}, f32[31,64,256]{2,1,0:T(8,128)}, ...), condition=%wide.region_22.23_spmd.clone, body=%wide.region_21.22_spmd.clone.sunk | while | flops 65539 | bytes 393823 | solution.py:36
  435.0 29.1 %while.226 = (s32[]{:T(128)}, f32[64,256]{1,0:T(8,128)S(1)}, f32[31,64,256]{2,1,0:T(8,128)S(1)}, f32[31,64,256]{2,1,0:T(8,128)}, f32[31,64,256]{2,1,0:T(8,128)}, /*index=5*/s32[]{:T(128)}, s32[]{:T(128)}, s32[]{:T(128)}) while((s32[]{:T(128)}, f32[64,256]{1,0:T(8,128)S(1)}, f32[31,64,256]{2,1,0:T(8,128)S(1)}, ...), condition=%wide.region_24.25_spmd.clone, body=%wide.region_23.24_spmd.clone.sunk | while | flops 49156 | bytes 327791 | solution.py:41
  466.0 48.3 %while.227 = (s32[]{:T(128)}, f32[64,256]{1,0:T(8,128)S(1)}, f32[31,64,256]{2,1,0:T(8,128)}, f32[31,64,256]{2,1,0:T(8,128)}, f32[31,64,256]{2,1,0:T(8,128)}, /*index=5*/f32[31,64,256]{2,1,0:T(8,128)}, s32[]{:T(128)}, s32[]{:T(128)}) while((s32[]{:T(128)}, f32[64,256]{1,0:T(8,128)S(1)}, f32[31,64,256]{2,1,0:T(8,128)}, ...), condition=%wide.region_26.27_spmd.clone, body=%wide.region_25.26_spmd.clone.sunk | while | flops 65539 | bytes 393823 | solution.py:36
  514.5 29.0 %while.228 = (s32[]{:T(128)}, f32[64,256]{1,0:T(8,128)S(1)}, f32[31,64,256]{2,1,0:T(8,128)S(1)}, f32[31,64,256]{2,1,0:T(8,128)}, f32[31,64,256]{2,1,0:T(8,128)}, /*index=5*/s32[]{:T(128)}, s32[]{:T(128)}, s32[]{:T(128)}) while((s32[]{:T(128)}, f32[64,256]{1,0:T(8,128)S(1)}, f32[31,64,256]{2,1,0:T(8,128)S(1)}, ...), condition=%wide.region_28.29_spmd.clone, body=%wide.region_27.28_spmd.clone.sunk | while | flops 49156 | bytes 327791 | solution.py:41
  546.8 48.8 %while.218 = (s32[]{:T(128)}, f32[64,256]{1,0:T(8,128)S(1)}, f32[31,64,256]{2,1,0:T(8,128)}, f32[31,64,256]{2,1,0:T(8,128)}, f32[31,64,256]{2,1,0:T(8,128)}, /*i...) while((s32[]{:T(128)}, f32[64,256]{1,0:T(8,128)S(1)}, ...), condition=%wide.region_6.7_spmd.clone, body=%wide.region_5.6_spmd.clone.sunk | while | flops 65539 | bytes 459367 | solution.py:27
  595.8 29.5 %while.219 = (s32[]{:T(128)}, f32[64,256]{1,0:T(8,128)S(1)}, f32[31,64,256]{2,1,0:T(8,128)S(1)}, f32[31,64,256]{2,1,0:T(8,128)}, f32[31,64,256]{2,1,0:T(8,128)},...) while((s32[]{:T(128)}, f32[64,256]{1,0:T(8,128)S(1)}, f32[31,64,256]{2,1,0:T(8,128)S(1)}, ...), condition=%wide.region_8.9_spmd.clone, body=%wide.region_7.8_spmd.clone.sunk | while | flops 65539 | bytes 393315 | solution.py:36
  626.9 29.0 %while.220 = (s32[]{:T(128)}, f32[64,256]{1,0:T(8,128)S(1)}, f32[31,64,256]{2,1,0:T(8,128)S(1)}, f32[31,64,256]{2,1,0:T(8,128)}, f32[31,64,256]{2,1,0:T(8,128)}, /*index=5*/s32[]{:T(128)}, s32[]{:T(128)}, s32[]{:T(128)}) while((s32[]{:T(128)}, f32[64,256]{1,0:T(8,128)S(1)}, f32[31,64,256]{2,1,0:T(8,128)S(1)}, ...), condition=%wide.region_10.11_spmd.clone, body=%wide.region_9.10_spmd.clone.sunk | while | flops 49156 | bytes 327791 | solution.py:41
  659.0 48.8 %while.221 = (s32[]{:T(128)}, f32[64,256]{1,0:T(8,128)S(1)}, f32[31,64,256]{2,1,0:T(8,128)}, f32[31,64,256]{2,1,0:T(8,128)}, f32[31,64,256]{2,1,0:T(8,128)}, /*i...) while((s32[]{:T(128)}, f32[64,256]{1,0:T(8,128)S(1)}, ...), condition=%wide.region_13.14_spmd.clone, body=%wide.region_12.13_spmd.clone.sunk | while | flops 65539 | bytes 459367 | solution.py:27
  709.4 48.3 %while.222 = (s32[]{:T(128)}, f32[64,256]{1,0:T(8,128)S(1)}, f32[31,64,256]{2,1,0:T(8,128)}, f32[31,64,256]{2,1,0:T(8,128)}, f32[31,64,256]{2,1,0:T(8,128)}, /*index=5*/f32[31,64,256]{2,1,0:T(8,128)}, s32[]{:T(128)}, s32[]{:T(128)}) while((s32[]{:T(128)}, f32[64,256]{1,0:T(8,128)S(1)}, f32[31,64,256]{2,1,0:T(8,128)}, ...), condition=%wide.region_15.16_spmd.clone, body=%wide.region_14.15_spmd.clone.sunk | while | flops 65539 | bytes 393823 | solution.py:36
  759.2 47.8 %while.223 = (s32[]{:T(128)}, f32[64,256]{1,0:T(8,128)S(1)}, f32[31,64,256]{2,1,0:T(8,128)}, f32[31,64,256]{2,1,0:T(8,128)}, f32[31,64,256]{2,1,0:T(8,128)}, /*index=5*/s32[]{:T(128)}, s32[]{:T(128)}, s32[]{:T(128)}) while((s32[]{:T(128)}, f32[64,256]{1,0:T(8,128)S(1)}, f32[31,64,256]{2,1,0:T(8,128)}, ...), condition=%wide.region_17.18_spmd.clone, body=%wide.region_16.17_spmd.clone.sunk | while | flops 49156 | bytes 327791 | solution.py:41
  810.1 440.8 %while.217 = (s32[]{:T(128)}, f32[64,256]{1,0:T(8,128)S(1)}, f32[64,256]{1,0:T(8,128)S(1)}, f32[64,256]{1,0:T(8,128)S(1)}, f32[64,256]{1,0:T(8,128)S(1)}, /*inde...) while((s32[]{:T(128)}, f32[64,256]{1,0:T(8,128)S(1)}, ...), condition=%wide.region_4.5_spmd.clone, body=%wide.region_3.4_spmd.clone.sunk | while | flops 491523 | bytes 1848143 | solution.py:134
  1255.2 20.8 %copy.124 = f32[31,10,1,256]{2,0,3,1:T(8,128)} copy(f32[31,10,1,256]{3,0,2,1:T(8,128)} %collective-permute-done.30) | data formatting | bytes 634880 | tf_op jit(solution)/shard_map/ppermute | solution.py:62
  1276.0 82.9 %fusion.31 = (f32[31,10,64,256]{2,0,3,1:T(8,128)}, f32[31,10,64,256]{2,0,3,1:T(8,128)}) fusion(f32[31,10,64,256]{2,0,3,1:T(8,128)} %copy.128, f32[31,10,1,256]{2,0,3,1:T(8,128)} %copy.124, f32[31,10,63,256]{2,0,3,1:T(8,128)} %slice.336, f32[31,64,256]{1,0,2:T(8,128)} %copy.120, pred[31,64,256]{1,0,2:T(8,128)(4,1)S(1)} %copy-done.29, ...), kind=kLoop, calls=%fused_computation.81 | loop fusion | flops 30474240 | bytes 106659840 | tf_op jit(solution)/shard_map/mul | solution.py:71
  1358.9 31.8 %slice.337 = f32[31,10,1,256]{2,0,3,1:T(8,128)} slice(f32[31,10,64,256]{2,0,3,1:T(8,128)} %get-tuple-element.1638), slice={[0:31], [0:10], [63:64], [0:256]} | slice | bytes 634880 | tf_op jit(solution)/shard_map/slice | solution.py:66
  1390.7 22.6 %copy.126 = f32[31,10,1,256]{3,0,2,1:T(8,128)S(1)} copy(f32[31,10,1,256]{2,0,3,1:T(8,128)} %slice.337) | data formatting | bytes 634880 | tf_op jit(solution)/shard_map/slice | solution.py:66
  1424.6 28.9 %slice.335 = f32[31,10,64,255]{2,0,3,1:T(8,128)} slice(f32[31,10,64,256]{2,0,3,1:T(8,128)} %get-tuple-element.1639), slice={[0:31], [0:10], [0:64], [0:255]} | slice | bytes 40473600 | tf_op jit(solution)/shard_map/slice | solution.py:59
  1453.5 20.1 %copy.127 = f32[31,10,1,256]{2,0,3,1:T(8,128)} copy(f32[31,10,1,256]{3,0,2,1:T(8,128)S(1)} %collective-permute-done.31) | data formatting | bytes 634880 | tf_op jit(solution)/shard_map/ppermute | solution.py:66
  1473.5 92.6 %fusion.30 = f32[31,10,64,256]{2,0,3,1:T(8,128)} fusion(f32[31,10,64,256]{2,0,3,1:T(8,128)} %copy.128, f32[31,10,64,256]{2,0,3,1:T(8,128)} %get-tuple-element.1639, f32[31,10,64,255]{2,0,3,1:T(8,128)} %slice.335, f32[31,10,64,1]{2,0,3,1:T(8,128)S(1)} %collective-permute-done.29, f32[31,10,64,256]{2,0,3,1:T(8,128)} %get-tuple-element.1638, ...), kind=kLoop, calls=%fused_computation.79 | loop fusion | flops 40632320 | bytes 123928576 | tf_op jit(solution)/shard_map/mul | solution.py:123
  1566.2 33.4 %copy.130 = f32[31,10,64,256]{3,2,1,0:T(8,128)} copy(f32[31,10,64,256]{2,0,3,1:T(8,128)} %fusion.30) | data formatting | bytes 40632320
  1599.5 9.4 broadcast.102.clone
  1609.0 95.9 %while.229 = (s32[]{:T(128)}, f32[10,64,256]{2,1,0:T(8,128)S(1)}, f32[31,10,64,256]{3,2,1,0:T(8,128)}, f32[31,10,64,256]{3,2,1,0:T(8,128)}, f32[31,64,256]{2,1,0...) while((s32[]{:T(128)}, f32[10,64,256]{2,1,0:T(8,128)S(1)}, ...), condition=%wide.region_30.31_spmd.clone, body=%wide.region_29.30_spmd.clone.sunk | while | flops 655363 | bytes 3015267 | solution.py:36
  1704.9 9.9 broadcast.102
  1714.8 94.9 %while.230 = (s32[]{:T(128)}, f32[10,64,256]{2,1,0:T(8,128)S(1)}, f32[31,10,64,256]{3,2,1,0:T(8,128)}, f32[31,10,64,256]{3,2,1,0:T(8,128)}, f32[31,64,256]{2,1,0:T(8,128)}, /*index=5*/s32[]{:T(128)}, s32[]{:T(128)}, s32[]{:T(128)}) while((s32[]{:T(128)}, f32[10,64,256]{2,1,0:T(8,128)S(1)}, f32[31,10,64,256]{3,2,1,0:T(8,128)}, ...), condition=%wide.region_32.33_spmd.clone, body=%wide.region_31.32_spmd.clone.sunk | while | flops 491524 | bytes 2818163 | solution.py:41
  1809.7 37.8 %copy.131 = f32[31,10,64,256]{2,0,3,1:T(8,128)} copy(f32[31,10,64,256]{3,2,1,0:T(8,128)} %get-tuple-element.1050) | data formatting | bytes 40632320 | tf_op jit(solution)/shard_map/while | solution.py:41
  1847.5 35.2 %broadcast_multiply_fusion = f32[31,10,64,256]{2,0,3,1:T(8,128)} fusion(f32[31,10,64,256]{2,0,3,1:T(8,128)} %copy.131, f32[31,64,256]{1,0,2:T(8,128)} %copy.129), kind=kLoop, calls=%fused_computation.83 | loop fusion | flops 5079040 | bytes 42663936 | tf_op jit(solution)/shard_map/mul | solution.py:123
  1882.7 33.4 %copy.132 = f32[31,10,64,256]{3,2,1,0:T(8,128)} copy(f32[31,10,64,256]{2,0,3,1:T(8,128)} %broadcast_multiply_fusion) | data formatting | bytes 40632320
  (1279 shorter events, 1315.7 us)
Async XLA Ops:
  1.5 142.5 %collective-permute-start.4 = (s32[64,1]{1,0:T(8,128)S(1)}, s32[64,1]{1,0:T(8,128)S(1)}, u32[]{:S(2)}, u32[]{:S(2)}) collective-permute-start(s32[64,1]{1,0:T(8,128)S(1)} %slice.225), channel_id=1, source_target_pairs={{0,8},{8,0},{1,9},{9,1},{2,10},{10,2},{3,11},{11,3},{4,12},{12,4},... | collective-permute-start | bytes 776 | tf_op jit(solution)/shard_map/ppermute | solution.py:54
  3.5 141.1 %collective-permute-start.5 = (s32[1,256]{1,0:T(1,128)S(1)}, s32[1,256]{1,0:T(1,128)}, u32[]{:S(2)}, u32[]{:S(2)}) collective-permute-start(s32[1,256]{1,0:T(1,128)S(1)} %slice.227), channel_id=1, source_target_pairs={{1,0},{2,1},{3,2},{4,3},{5,4},{6,5},{7,6},{9,8},{10,9},{11,10},{12... | collective-permute-start | bytes 3080 | tf_op jit(solution)/shard_map/ppermute | solution.py:62
  7.3 191.2 %collective-permute-start.20 = (f32[31,64,1]{1,2,0:T(1,128)}, f32[31,64,1]{1,2,0:T(1,128)}, u32[]{:S(2)}, u32[]{:S(2)}) collective-permute-start(f32[31,64,1]{1,2,0:T(1,128)} %copy.133), channel_id=1, source_target_pairs={{0,8},{8,0},{1,9},{9,1},{2,10},{10,2},{3,11},{11,3},{4,12},{12,4},... | collective-permute-start | bytes 23816 | tf_op jit(solution)/shard_map/ppermute | solution.py:54
  7.9 194.6 %collective-permute-start.24 = (f32[31,64,1]{1,2,0:T(1,128)S(1)}, f32[31,64,1]{1,2,0:T(1,128)}, u32[]{:S(2)}, u32[]{:S(2)}) collective-permute-start(f32[31,64,1]{1,2,0:T(1,128)S(1)} %copy.134), channel_id=1, source_target_pairs={{0,8},{8,0},{1,9},{9,1},{2,10},{10,2},{3,11},{11,3},{4,12},{12,4},... | collective-permute-start | bytes 23816 | tf_op jit(solution)/shard_map/ppermute | solution.py:54
  143.8 61.1 %collective-permute-start.14 = (f32[31,64,1]{1,2,0:T(1,128)}, f32[31,64,1]{1,2,0:T(1,128)}, u32[]{:S(2)}, u32[]{:S(2)}) collective-permute-start(f32[31,64,1]{1,2,0:T(1,128)} %copy.103), channel_id=1, source_target_pairs={{0,8},{8,0},{1,9},{9,1},{2,10},{10,2},{3,11},{11,3},{4,12},{12,4},... | collective-permute-start | bytes 23816 | tf_op jit(solution)/shard_map/ppermute | solution.py:54
  167.6 40.7 %collective-permute-start.9 = (f32[31,64,1]{1,2,0:T(1,128)}, f32[31,64,1]{1,2,0:T(1,128)}, u32[]{:S(2)}, u32[]{:S(2)}) collective-permute-start(f32[31,64,1]{1,2,0:T(1,128)} %copy.101), channel_id=1, source_target_pairs={{0,8},{8,0},{1,9},{9,1},{2,10},{10,2},{3,11},{11,3},{4,12},{12,4},... | collective-permute-start | bytes 23816 | tf_op jit(solution)/shard_map/ppermute | solution.py:54
  195.5 23.3 %collective-permute-start.22 = (f32[31,1,256]{2,1,0:T(1,128)}, f32[31,1,256]{2,1,0:T(1,128)}, u32[]{:S(2)}, u32[]{:S(2)}) collective-permute-start(f32[31,1,256]{2,1,0:T(1,128)} %slice.261), channel_id=1, source_target_pairs={{1,0},{2,1},{3,2},{4,3},{5,4},{6,5},{7,6},{9,8},{10,9},{11,10},{12... | collective-permute-start | bytes 95240 | tf_op jit(solution)/shard_map/ppermute | solution.py:62
  200.6 18.2 collective-permute-start.26
  204.7 8.2 collective-permute-start.8
  207.0 36.1 %collective-permute-start.7 = (f32[31,64,1]{1,2,0:T(1,128)}, f32[31,64,1]{1,2,0:T(1,128)}, u32[]{:S(2)}, u32[]{:S(2)}) collective-permute-start(f32[31,64,1]{1,2,0:T(1,128)} %copy.97), channel_id=1, source_target_pairs={{0,8},{8,0},{1,9},{9,1},{2,10},{10,2},{3,11},{11,3},{4,12},{12,4},... | collective-permute-start | bytes 23816 | tf_op jit(solution)/shard_map/ppermute | solution.py:54
  212.7 35.0 %collective-permute-start.17 = (f32[31,64,1]{1,2,0:T(1,128)S(1)}, f32[31,64,1]{1,2,0:T(1,128)}, u32[]{:S(2)}, u32[]{:S(2)}) collective-permute-start(f32[31,64,1]{1,2,0:T(1,128)S(1)} %copy-done.61), channel_id=1, source_target_pairs={{0,8},{8,0},{1,9},{9,1},{2,10},{10,2},{3,11},{11,3},{4,12},{12,4},... | collective-permute-start | bytes 23816 | tf_op jit(solution)/shard_map/ppermute | solution.py:58
  231.7 17.9 collective-permute-start.21
  237.7 13.9 collective-permute-start.25
  239.7 26.0 %collective-permute-start.19 = (f32[31,1,256]{2,1,0:T(1,128)}, f32[31,1,256]{2,1,0:T(1,128)}, u32[]{:S(2)}, u32[]{:S(2)}) collective-permute-start(f32[31,1,256]{2,1,0:T(1,128)} %slice.323), channel_id=1, source_target_pairs={{1,0},{2,1},{3,2},{4,3},{5,4},{6,5},{7,6},{9,8},{10,9},{11,10},{12... | collective-permute-start | bytes 95240 | tf_op jit(solution)/shard_map/ppermute | solution.py:62
  243.1 23.8 %collective-permute-start.10 = (f32[31,1,256]{2,1,0:T(1,128)}, f32[31,1,256]{2,1,0:T(1,128)}, u32[]{:S(2)}, u32[]{:S(2)}) collective-permute-start(f32[31,1,256]{2,1,0:T(1,128)} %get-tuple-element.1651), channel_id=1, source_target_pairs={{0,1},{1,2},{2,3},{3,4},{4,5},{5,6},{6,7},{8,9},{9,10},{10,11},{11... | collective-permute-start | bytes 95240 | tf_op jit(solution)/shard_map/ppermute | solution.py:66
  247.7 21.2 %collective-permute-start.12 = (f32[31,1,256]{2,1,0:T(1,128)}, f32[31,1,256]{2,1,0:T(1,128)}, u32[]{:S(2)}, u32[]{:S(2)}) collective-permute-start(f32[31,1,256]{2,1,0:T(1,128)} %get-tuple-element.1658), channel_id=1, source_target_pairs={{1,0},{2,1},{3,2},{4,3},{5,4},{6,5},{7,6},{9,8},{10,9},{11,10},{12... | collective-permute-start | bytes 95240 | tf_op jit(solution)/shard_map/ppermute | solution.py:62
  249.6 24.1 %collective-permute-start.18 = (f32[31,1,256]{2,1,0:T(1,128)}, f32[31,1,256]{2,1,0:T(1,128)}, u32[]{:S(2)}, u32[]{:S(2)}) collective-permute-start(f32[31,1,256]{2,1,0:T(1,128)} %get-tuple-element.1650), channel_id=1, source_target_pairs={{1,0},{2,1},{3,2},{4,3},{5,4},{6,5},{7,6},{9,8},{10,9},{11,10},{12... | collective-permute-start | bytes 95240 | tf_op jit(solution)/shard_map/ppermute | solution.py:62
  251.5 24.5 %collective-permute-start.16 = (f32[31,1,256]{2,1,0:T(1,128)}, f32[31,1,256]{2,1,0:T(1,128)}, u32[]{:S(2)}, u32[]{:S(2)}) collective-permute-start(f32[31,1,256]{2,1,0:T(1,128)} %fusion.73), channel_id=1, source_target_pairs={{1,0},{2,1},{3,2},{4,3},{5,4},{6,5},{7,6},{9,8},{10,9},{11,10},{12... | collective-permute-start | bytes 95240 | tf_op jit(solution)/shard_map/ppermute | solution.py:62
  265.7 1010.2 %collective-permute-start.28 = (f32[31,10,64,1]{2,0,3,1:T(8,128)}, f32[31,10,64,1]{2,0,3,1:T(8,128)}, u32[]{:S(2)}, u32[]{:S(2)}) collective-permute-start(f32[31,10,64,1]{2,0,3,1:T(8,128)} %slice.333), channel_id=1, source_target_pairs={{0,8},{8,0},{1,9},{9,1},{2,10},{10,2},{3,11},{11,3},{4,12},{12,4},... | collective-permute-start | bytes 238088 | tf_op jit(solution)/shard_map/ppermute | solution.py:54
  266.9 988.3 %collective-permute-start.30 = (f32[31,10,1,256]{3,0,2,1:T(8,128)}, f32[31,10,1,256]{3,0,2,1:T(8,128)}, u32[]{:S(2)}, u32[]{:S(2)}) collective-permute-start(f32[31,10,1,256]{3,0,2,1:T(8,128)} %copy.135), channel_id=1, source_target_pairs={{1,0},{2,1},{3,2},{4,3},{5,4},{6,5},{7,6},{9,8},{10,9},{11,10},{12... | collective-permute-start | bytes 952328 | tf_op jit(solution)/shard_map/ppermute | solution.py:62
  268.8 34.3 %collective-permute-start.13 = (f32[31,1,256]{2,1,0:T(1,128)}, f32[31,1,256]{2,1,0:T(1,128)S(1)}, u32[]{:S(2)}, u32[]{:S(2)}) collective-permute-start(f32[31,1,256]{2,1,0:T(1,128)} %get-tuple-element.1659), channel_id=1, source_target_pairs={{0,1},{1,2},{2,3},{3,4},{4,5},{5,6},{6,7},{8,9},{9,10},{10,11},{11... | collective-permute-start | bytes 95240 | tf_op jit(solution)/shard_map/ppermute | solution.py:66
  273.7 32.6 %collective-permute-start.11 = (f32[31,1,256]{2,1,0:T(1,128)}, f32[31,1,256]{2,1,0:T(1,128)S(1)}, u32[]{:S(2)}, u32[]{:S(2)}) collective-permute-start(f32[31,1,256]{2,1,0:T(1,128)} %fusion.72), channel_id=1, source_target_pairs={{0,1},{1,2},{2,3},{3,4},{4,5},{5,6},{6,7},{8,9},{9,10},{10,11},{11... | collective-permute-start | bytes 95240 | tf_op jit(solution)/shard_map/ppermute | solution.py:66
  299.5 19.3 %collective-permute-start.23 = (f32[31,1,256]{2,1,0:T(1,128)}, f32[31,1,256]{2,1,0:T(1,128)}, u32[]{:S(2)}, u32[]{:S(2)}) collective-permute-start(f32[31,1,256]{2,1,0:T(1,128)} %slice.326), channel_id=1, source_target_pairs={{0,1},{1,2},{2,3},{3,4},{4,5},{5,6},{6,7},{8,9},{9,10},{10,11},{11... | collective-permute-start | bytes 95240 | tf_op jit(solution)/shard_map/ppermute | solution.py:66
  303.2 17.6 collective-permute-start.27
  318.5 490.5 %collective-permute-start.6 = (f32[64,1]{1,0:T(8,128)}, f32[64,1]{1,0:T(8,128)}, u32[]{:S(2)}, u32[]{:S(2)}) collective-permute-start(f32[64,1]{1,0:T(8,128)} %slice.293), channel_id=1, source_target_pairs={{0,8},{8,0},{1,9},{9,1},{2,10},{10,2},{3,11},{11,3},{4,12},{12,4},... | collective-permute-start | bytes 776 | tf_op jit(solution)/shard_map/ppermute | solution.py:54
  318.8 490.2 %collective-permute-start.15 = (f32[1,256]{1,0:T(1,128)S(1)}, f32[1,256]{1,0:T(1,128)S(1)}, u32[]{:S(2)}, u32[]{:S(2)}) collective-permute-start(f32[1,256]{1,0:T(1,128)S(1)} %copy-done.62), channel_id=1, source_target_pairs={{1,0},{2,1},{3,2},{4,3},{5,4},{6,5},{7,6},{9,8},{10,9},{11,10},{12... | collective-permute-start | bytes 3080 | tf_op jit(solution)/shard_map/ppermute | solution.py:62
  824.2 8.0 collective-permute-start.1
  838.9 8.0 collective-permute-start.1
  853.6 8.0 collective-permute-start.1
  868.3 8.0 collective-permute-start.1
  1413.3 40.2 %collective-permute-start.31 = (f32[31,10,1,256]{3,0,2,1:T(8,128)S(1)}, f32[31,10,1,256]{3,0,2,1:T(8,128)S(1)}, u32[]{:S(2)}, u32[]{:S(2)}) collective-permute-start(f32[31,10,1,256]{3,0,2,1:T(8,128)S(1)} %copy.126), channel_id=1, source_target_pairs={{0,1},{1,2},{2,3},{3,4},{4,5},{5,6},{6,7},{8,9},{9,10},{10,11},{11... | collective-permute-start | bytes 952328 | tf_op jit(solution)/shard_map/ppermute | solution.py:66
  1419.4 54.1 %collective-permute-start.29 = (f32[31,10,64,1]{2,0,3,1:T(8,128)S(1)}, f32[31,10,64,1]{2,0,3,1:T(8,128)S(1)}, u32[]{:S(2)}, u32[]{:S(2)}) collective-permute-start(f32[31,10,64,1]{2,0,3,1:T(8,128)S(1)} %slice.334), channel_id=1, source_target_pairs={{0,8},{8,0},{1,9},{9,1},{2,10},{10,2},{3,11},{11,3},{4,12},{12,4},... | collective-permute-start | bytes 238088 | tf_op jit(solution)/shard_map/ppermute | solution.py:58
  (185 other events, 1496.5 us)
where the time goes:
time: 1950 us; the launch traced here: 1920 us
  other arithmetic  916 us (47%)
  local copies, waits for them, and re-layouts  549 us (28%)
  starting transfers between devices  336 us (17%)
  waiting for transfers between devices  110 us (6%)
    dynamic_update_slice x310, other arithmetic, tridiag_apply(): lax.scan(fwd_step, jnp.zeros_like(rhs_all[0]), (sub_diag, pivots, rhs_all))  444 us
    ppermute x36, starting transfers between devices, shift_south(): edge_strip = lax.ppermute(grid_field[..., -1:, :], 'row', to_north)  179 us
    dynamic_update_slice x93, other arithmetic, tridiag_factor(): lax.scan(value_a9, jnp.zeros_like(main_diag[0]), (sub_diag, main_diag, su...  146 us
    unnamed x138, local copies, waits for them, and re-layouts  113 us
    mul x1, other arithmetic, local_step(): advect_tracer(tracers, u_face[:, None], v_face[:, None]) * mask_t  92.6 us
    mul x2, other arithmetic, advect_tracer(): v_face * jnp.where(v_face > 0, tracer_field, shift_north(tracer_field))  90.9 us
    ppermute x39, starting transfers between devices, shift_north(): edge_strip = lax.ppermute(grid_field[..., :1, :], 'row', to_south)  78.3 us
    slice x34, local copies, waits for them, and re-layouts, shift_south(): edge_strip = lax.ppermute(grid_field[..., -1:, :], 'row', to_north)  57.6 us
  transfers between devices with their start and end apart: 148, of which 90 were waited for; matrix products, arithmetic and copies ran while one was open for 46% of the time, Pallas kernels for 0%

commit v1 on v0

v1 whole, which is shorter than its diff:
```python
import functools

import jax
import jax.numpy as jnp
import numpy as np
from jax import lax
from jax.experimental import pallas as pl
from jax.experimental.pallas import tpu as pltpu
from jax.sharding import PartitionSpec as P

GRAV_ACC = 400.0
DT_STEP = 0.4
THERMAL_EXP = 0.002
HALINE_CON = 0.004
R_VISC = 2.0
R_DIFF = 0.5

LEV = 31
ROWS = 64
LANES = 128
NTR = 10
NSUB = 30
DTB = DT_STEP / NSUB
HALO = 32
BASE = 40
EROWS = 144
PROWS = 80
MESH = pl.DeviceIdType.MESH
F32 = jnp.float32


def pivot_tables(r_coef):
    mid, last = [], []
    prev = None
    for k in range(LEV):
        if k == 0:
            p_mid, p_last = 1.0 + r_coef, 1.0
        else:
            p_mid = 1.0 + 2.0 * r_coef - r_coef * r_coef / prev
            p_last = 1.0 + r_coef - r_coef * r_coef / prev
        mid.append(1.0 / p_mid)
        last.append(1.0 / p_last)
        prev = p_mid
    return mid, last


VISC_MID, VISC_LAST = pivot_tables(R_VISC)
DIFF_MID, DIFF_LAST = pivot_tables(R_DIFF)


def lane_iota(rows):
    return lax.broadcasted_iota(jnp.int32, (rows, LANES), 1)


def inv_pivot(count, k, mid, last):
    kf = float(k)
    return jnp.where(count > kf, jnp.where(count > kf + 1.0, mid[k], last[k]), 0.0)


def momentum_kernel(
    num_col, num_row,
    u_hbm, v_hbm, t_hbm, s_hbm, tr_hbm, eta_hbm, tu_hbm, tv_hbm, bot_hbm, kmt_hbm, w_ref,
    pred_hbm, geo_ref, bt_ref, hn_hbm, hs_hbm, hts_hbm, ew_hbm, uw_hbm, vs_hbm,
    x3, pres, tend, tbuf, ext, comb, geom, kint, cum, force, avg, ews, ewr,
    lsem, tsem, osem, ssem, rsem,
):
    col = lax.axis_index("col")
    row = lax.axis_index("row")
    oth = lax.rem(col + 1, num_col)
    dev_s, dev_n = (col, row - 1), (col, row + 1)
    dev_o, dev_so, dev_no = (oth, row), (oth, row - 1), (oth, row + 1)
    has_s = row > 0
    has_n = row < num_row - 1

    fields2d = (bot_hbm, eta_hbm, tu_hbm, tv_hbm)
    reads2d = []
    for t in range(2):
        lanes = pl.ds(t * LANES, LANES)
        reads2d.append(pltpu.make_async_copy(kmt_hbm.at[:, lanes], kint.at[t], lsem.at[0, t]))
        for i, ref in enumerate(fields2d):
            reads2d.append(
                pltpu.make_async_copy(ref.at[:, lanes], ext.at[1 + i, t, pl.ds(BASE, ROWS), :], lsem.at[1 + i, t])
            )
    reads3d = []
    for f, ref in enumerate((u_hbm, v_hbm, t_hbm, s_hbm)):
        for t in range(2):
            lanes = pl.ds(t * LANES, LANES)
            reads3d.append(
                pltpu.make_async_copy(ref.at[:, :, lanes], x3.at[f, :, t, pl.ds(8, ROWS), :], lsem.at[5 + f, t])
            )
    for cp in reads2d + reads3d:
        cp.start()

    def tracer_read(p):
        return pltpu.make_async_copy(tr_hbm.at[:, pl.ds(2 * p, 2)], tbuf.at[p % 2], tsem.at[p % 2])

    tracer_read(0).start()
    tracer_read(1).start()

    barrier = pltpu.get_barrier_semaphore()
    pl.semaphore_signal(barrier, inc=1, device_id=dev_o, device_id_type=MESH)

    @pl.when(has_s)
    def _():
        pl.semaphore_signal(barrier, inc=1, device_id=dev_s, device_id_type=MESH)
        pl.semaphore_signal(barrier, inc=1, device_id=dev_so, device_id_type=MESH)

    @pl.when(has_n)
    def _():
        pl.semaphore_signal(barrier, inc=1, device_id=dev_n, device_id_type=MESH)
        pl.semaphore_signal(barrier, inc=1, device_id=dev_no, device_id_type=MESH)

    def remote(i, src, dst, dev):
        return pltpu.make_async_remote_copy(
            src_ref=src, dst_ref=dst, send_sem=ssem.at[i], recv_sem=rsem.at[i], device_id=dev, device_id_type=MESH
        )

    lo, hi = pl.ds(BASE, HALO), pl.ds(BASE + ROWS - HALO, HALO)
    above, below = pl.ds(BASE + ROWS, HALO), pl.ds(BASE - HALO, HALO)
    own = pl.ds(BASE, ROWS)

    def plane_copies(first, f0, n):
        fs = pl.ds(f0, n)
        two = pl.ds(0, 2)
        return (
            (remote(first, ext.at[fs, two, lo, :], ext.at[fs, two, above, :], dev_s), "s"),
            (remote(first + 1, ext.at[fs, two, hi, :], ext.at[fs, two, below, :], dev_n), "n"),
            (remote(first + 2, comb.at[fs], ext.at[fs, 2, own, :], dev_o), "o"),
            (remote(first + 3, comb.at[fs, pl.ds(0, HALO), :], ext.at[fs, 2, above, :], dev_so), "s"),
            (remote(first + 4, comb.at[fs, pl.ds(ROWS - HALO, HALO), :], ext.at[fs, 2, below, :], dev_no), "n"),
        )

    def edge_copies(first, f0):
        fs, two = pl.ds(f0, 2), pl.ds(0, 2)
        return (
            (remote(first, x3.at[fs, :, two, pl.ds(8, 1), :], x3.at[fs, :, two, pl.ds(72, 1), :], dev_s), "s"),
            (remote(first + 1, x3.at[fs, :, two, pl.ds(71, 1), :], x3.at[fs, :, two, pl.ds(7, 1), :], dev_n), "n"),
        )

    geo_copies = plane_copies(0, 0, 2)
    state_copies = plane_copies(5, 2, 3)
    force_copies = plane_copies(10, 5, 2)
    uv_copies = edge_copies(15, 0) + (
        (remote(17, x3.at[0, :, 1, pl.ds(8, 1), :], x3.at[0, :, 2, pl.ds(72, 1), :], dev_so), "s"),
        (remote(18, x3.at[1, :, 0, pl.ds(71, 1), :], x3.at[1, :, 2, pl.ds(7, 1), :], dev_no), "n"),
    )
    ts_copies = edge_copies(19, 2)
    ew_copies = [((remote(21, ews.at[0], ewr.at[0], dev_o), "o"),), ((remote(22, ews.at[1], ewr.at[1], dev_o), "o"),)]
    for p in range(NTR // 2):
        ew_copies.append(((remote(23 + p, ews.at[2 + p], ew_hbm.at[1 + p], dev_o), "o"),))
    tr_copies = (
        (remote(28, tr_hbm.at[:, :, pl.ds(0, 1), :], hn_hbm, dev_s), "s"),
        (remote(29, tr_hbm.at[:, :, pl.ds(ROWS - 1, 1), :], hs_hbm, dev_n), "n"),
    )

    def run_by_side(copies, action, receiving):
        for side, cond in (("o", None), ("s", has_n if receiving else has_s), ("n", has_s if receiving else has_n)):
            picked = [cp for cp, s in copies if s == side]
            if not picked:
                continue
            if cond is None:
                for cp in picked:
                    action(cp)
            else:

                @pl.when(cond)
                def _(picked=picked):
                    for cp in picked:
                        action(cp)

    def start(copies):
        run_by_side(copies, lambda cp: cp.start(), False)

    def wait_recv(copies):
        run_by_side(copies, lambda cp: cp.wait_recv(), True)

    def wait_send(copies):
        run_by_side(copies, lambda cp: cp.wait_send(), False)

    def zero_wall(rows2d, row3d):
        for f in range(7):
            for t in range(3):
                ext[f, t, rows2d, :] = jnp.zeros((HALO, LANES), F32)

        def body(k, carry):
            for f in range(4):
                for t in range(3):
                    x3[f, k, t, pl.ds(row3d, 1), :] = jnp.zeros((1, LANES), F32)
            return carry

        lax.fori_loop(0, LEV, body, 0)

    @pl.when(jnp.logical_not(has_s))
    def _():
        zero_wall(below, 7)

    @pl.when(jnp.logical_not(has_n))
    def _():
        zero_wall(above, 72)

    for cp in reads2d:
        cp.wait()
    half = lane_iota(ROWS) < LANES // 2
    for t in range(2):
        ext[0, t, own, :] = kint[t].astype(F32)
    for f in range(5):
        comb[f] = jnp.where(half, ext[f, 0, own, :], ext[f, 1, own, :])

    pl.semaphore_wait(barrier, 1 + 2 * has_s.astype(jnp.int32) + 2 * has_n.astype(jnp.int32))

    for cp in reads3d[:4]:
        cp.wait()
    start(uv_copies)
    start(geo_copies)

    lane = lane_iota(ROWS)
    slab_of_lane = lane // 2

    def pack(group, load):
        acc = jnp.zeros((ROWS, LANES), F32)
        for f in range(2):

            def body(k, acc, f=f):
                slab = k + f * LEV
                left, right = load(f, k)
                edge = pltpu.roll(jnp.where(half, left, right), 2 * slab + 1, 1)
                return jnp.where(slab_of_lane == slab, edge, acc)

            acc = lax.fori_loop(0, LEV, body, acc)
        ews[group] = acc

    rows3 = pl.ds(8, ROWS)
    pack(0, lambda f, k: (x3[f, k, 0, rows3, :], x3[f, k, 1, rows3, :]))
    for cp in reads3d[4:]:
        cp.wait()
    start(ew_copies[0])
    start(ts_copies)
    pack(1, lambda f, k: (x3[2 + f, k, 0, rows3, :], x3[2 + f, k, 1, rows3, :]))
    start(state_copies)
    for p in range(NTR // 2):
        tracer_read(p).wait()
        start(ew_copies[1 + p])
        if p == 0:
            start(tr_copies)
        slot = p % 2
        pack(
            2 + p,
            lambda f, k: (tbuf[slot, k, f, :, pl.ds(0, LANES)], tbuf[slot, k, f, :, pl.ds(LANES, LANES)]),
        )
        if p + 2 < NTR // 2:
            tracer_read(p + 2).start()

    wait_recv(geo_copies)
    start(ew_copies[1 + NTR // 2])
    chunk = 32
    first_lane, last_lane = lane_iota(chunk) == 0, lane_iota(chunk) == LANES - 1

    def east(tiles, n=3):
        rolled = [pltpu.roll(x, LANES - 1, 1) for x in tiles]
        edge = last_lane if tiles[0].shape[0] == chunk else lane_iota(tiles[0].shape[0]) == LANES - 1
        return [jnp.where(edge, rolled[(t + 1) % 3], rolled[t]) for t in range(n)]

    def west(tiles, n=3):
        rolled = [pltpu.roll(x, 1, 1) for x in tiles]
        edge = first_lane if tiles[0].shape[0] == chunk else lane_iota(tiles[0].shape[0]) == 0
        return [jnp.where(edge, rolled[(t + 2) % 3], rolled[t]) for t in range(n)]

    def thickness(count, bottom):
        return jnp.where(count > 0.0, bottom / jnp.maximum(count, 1.0), 0.0)

    for c in range(8, 8 + ROWS + 2 * HALO, chunk):
        rs, rn = pl.ds(c, chunk), pl.ds(c + 1, chunk)
        kc = [ext[0, t, rs, :] for t in range(3)]
        hc = [thickness(kc[t], ext[1, t, rs, :]) for t in range(3)]
        kn = [ext[0, t, rn, :] for t in range(3)]
        hn = [thickness(kn[t], ext[1, t, rn, :]) for t in range(3)]
        ke, he = east(kc), east(hc)
        for t in range(3):
            ku, kv = jnp.minimum(kc[t], ke[t]), jnp.minimum(kc[t], kn[t])
            geom[0, t, rs, :] = ku
            geom[1, t, rs, :] = kv
            geom[2, t, rs, :] = (DTB * DTB * GRAV_ACC) * (ku * jnp.minimum(hc[t], he[t]))
            geom[3, t, rs, :] = (DTB * DTB * GRAV_ACC) * (kv * jnp.minimum(hc[t], hn[t]))
            geom[4, t, rs, :] = jnp.where(kc[t] > 0.0, 1.0, 0.0)
            geom[5, t, rs, :] = GRAV_ACC * hc[t]

    wait_send(uv_copies)
    wait_recv(uv_copies)
    wait_recv(ts_copies)
    wait_recv(ew_copies[0])
    wait_recv(ew_copies[1])
    for t in range(3):
        cum[t] = jnp.zeros((PROWS, LANES), F32)
    gr = BASE - 8

    def mask_level(k, carry):
        kf = k.astype(F32)
        for f in range(2):
            for t in range(2):
                x3[f, k, t] = jnp.where(kf < geom[f, t, pl.ds(gr, PROWS), :], x3[f, k, t], 0.0)
            edge = pltpu.roll(ewr[0], 2 * LANES - 1 - 2 * (k + f * LEV), 1)
            x3[f, k, 2, rows3, :] = jnp.where(kf < geom[f, 2, own, :], edge, 0.0)
            corner = 72 if f == 0 else 0
            x3[f, k, 2, pl.ds(corner, 8), :] = jnp.where(
                kf < geom[f, 2, pl.ds(gr + corner, 8), :], x3[f, k, 2, pl.ds(corner, 8), :], 0.0
            )
        for t in range(3):
            rs = pl.ds(8, 72) if t < 2 else rows3
            if t < 2:
                tt, ss = x3[2, k, t, rs, :], x3[3, k, t, rs, :]
            else:
                tt = pltpu.roll(ewr[1], 2 * LANES - 1 - 2 * k, 1)
                ss = pltpu.roll(ewr[1], 2 * LANES - 1 - 2 * (k + LEV), 1)
            rho = HALINE_CON * ss - THERMAL_EXP * tt
            total = cum[t, rs, :] + rho
            cum[t, rs, :] = total
            pres[k, t, rs, :] = geom[5, t, pl.ds(BASE, rs.size), :] * (total - 0.5 * rho)
        return carry

    lax.fori_loop(0, LEV, mask_level, 0)

    outs = [
        pltpu.make_async_copy(x3.at[0, :, 2, rows3, :], uw_hbm, osem.at[0]),
        pltpu.make_async_copy(x3.at[1, :, pl.ds(0, 2), pl.ds(7, 1), :], vs_hbm, osem.at[1]),
        pltpu.make_async_copy(x3.at[pl.ds(2, 2), :, pl.ds(0, 2), pl.ds(72, 1), :], hts_hbm.at[0], osem.at[2]),
        pltpu.make_async_copy(x3.at[pl.ds(2, 2), :, pl.ds(0, 2), pl.ds(7, 1), :], hts_hbm.at[1], osem.at[3]),
        pltpu.make_async_copy(ewr.at[1], ew_hbm.at[0], osem.at[4]),
    ]
    for cp in outs:
        cp.start()

    for f in range(2):
        for t in range(2):
            force[f, t] = jnp.zeros((ROWS, LANES), F32)

    def tend_level(k, carry):
        kf = k.astype(F32)
        for c in range(0, ROWS, chunk):
            rs, rn, rb = pl.ds(8 + c, chunk), pl.ds(9 + c, chunk), pl.ds(7 + c, chunk)
            uc = [x3[0, k, t, rs, :] for t in range(3)]
            vc = [x3[1, k, t, rs, :] for t in range(3)]
            un = [x3[0, k, t, rn, :] for t in range(3)]
            vb = [x3[1, k, t, rb, :] for t in range(3)]
            pc = [pres[k, t, rs, :] for t in range(3)]
            ue, uw, ve, vw = east(uc, 2), west(uc, 2), east(vc, 2), west(vc, 2)
            unw, vbe, pe = west(un, 2), east(vb, 2), east(pc, 2)
            for t in range(2):
                ub = x3[0, k, t, rb, :]
                vn = x3[1, k, t, rn, :]
                pn = pres[k, t, rn, :]
                va = (vc[t] + ve[t]) + (vb[t] + vbe[t])
                ua = (uc[t] + uw[t]) + (un[t] + unw[t])
                gu = -0.5 * (uc[t] * (ue[t] - uw[t])) - 0.125 * (va * (un[t] - ub)) - (pe[t] - pc[t])
                gv = -0.125 * (ua * (ve[t] - vw[t])) - 0.5 * (vc[t] * (vn - vb[t])) - (pn - pc[t])
                gs = pl.ds(BASE + c, chunk)
                gu = jnp.where(kf < geom[0, t, gs, :], gu, 0.0)
                gv = jnp.where(kf < geom[1, t, gs, :], gv, 0.0)
                cs = pl.ds(c, chunk)
                tend[0, k, t, cs, :] = uc[t] + DT_STEP * gu
                tend[1, k, t, cs, :] = vc[t] + DT_STEP * gv
                force[0, t, cs, :] += gu
                force[1, t, cs, :] += gv
        return carry

    lax.fori_loop(0, LEV, tend_level, 0)

    def face_thickness(c):
        rs, rn = pl.ds(BASE + c, chunk), pl.ds(BASE + c + 1, chunk)
        hc = [thickness(ext[0, t, rs, :], ext[1, t, rs, :]) for t in range(3)]
        he = east(hc, 2)
        hn = [thickness(ext[0, t, rn, :], ext[1, t, rn, :]) for t in range(2)]
        return [jnp.minimum(hc[t], he[t]) for t in range(2)], [jnp.minimum(hc[t], hn[t]) for t in range(2)]

    for c in range(0, ROWS, chunk):
        hu, hv = face_thickness(c)
        cs = pl.ds(c, chunk)
        for f, hf in ((0, hu), (1, hv)):
            scaled = [(DTB * DTB) * (hf[t] * force[f, t, cs, :]) for t in range(2)]
            for t in range(2):
                ext[5 + f, t, pl.ds(BASE + c, chunk), :] = scaled[t]
            comb[5 + f, cs, :] = jnp.where(lane_iota(chunk) < LANES // 2, scaled[0], scaled[1])

    wait_recv(state_copies)
    wait_send(state_copies)
    for c in range(8, 8 + ROWS + 2 * HALO, chunk):
        rs = pl.ds(c, chunk)
        for t in range(3):
            ext[2, t, rs, :] = ext[2, t, rs, :] * geom[4, t, rs, :]
            for f in range(2):
                ext[3 + f, t, rs, :] = jnp.where(geom[f, t, rs, :] > 0.0, DTB * ext[3 + f, t, rs, :], 0.0)
    start(force_copies)

    def solve_rows(b, carry):
        r0 = pl.multiple_of(b * 8, 8)
        rs = pl.ds(r0, 8)
        count = [[geom[f, t, pl.ds(pl.multiple_of(BASE + b * 8, 8), 8), :] for t in range(2)] for f in range(2)]
        prev = [[jnp.zeros((8, LANES), F32)] * 2 for f in range(2)]
        for k in range(LEV):
            for f in range(2):
                for t in range(2):
                    inv = inv_pivot(count[f][t], k, VISC_MID, VISC_LAST)
                    rhs = tend[f, k, t, rs, :]
                    prev[f][t] = (rhs + R_VISC * prev[f][t]) * inv if k else rhs * inv
                    tend[f, k, t, rs, :] = prev[f][t]
        total = [[prev[f][t] for t in range(2)] for f in range(2)]
        for k in range(LEV - 2, -1, -1):
            for f in range(2):
                for t in range(2):
                    prev[f][t] = tend[f, k, t, rs, :] + (R_VISC * VISC_MID[k]) * prev[f][t]
                    total[f][t] = total[f][t] + prev[f][t]
                    tend[f, k, t, rs, :] = prev[f][t]
        for f in range(2):
            for t in range(2):
                force[f, t, rs, :] = total[f][t] / jnp.maximum(count[f][t], 1.0)
        return carry

    lax.fori_loop(0, ROWS // 8, solve_rows, 0)
    pred_out = pltpu.make_async_copy(tend, pred_hbm, osem.at[5])
    pred_out.start()

    for f in range(2):
        for t in range(2):
            avg[f, t] = jnp.zeros((ROWS, LANES), F32)
    wait_recv(force_copies)

    def subcycle(n, carry):
        wn = w_ref[n]
        for c in range(8, 8 + ROWS + 2 * HALO, chunk):
            rs, rb = pl.ds(c, chunk), pl.ds(c - 1, chunk)
            uc = [ext[3, t, rs, :] for t in range(3)]
            uw = west(uc)
            for t in range(3):
                div = (uc[t] - uw[t]) + (ext[4, t, rs, :] - ext[4, t, rb, :])
                ext[2, t, rs, :] = (ext[2, t, rs, :] - div) * geom[4, t, rs, :]
        for c in range(8, 8 + ROWS + 2 * HALO, chunk):
            rs, rn = pl.ds(c, chunk), pl.ds(c + 1, chunk)
            ec = [ext[2, t, rs, :] for t in range(3)]
            ee = east(ec)
            for t in range(3):
                un = ext[3, t, rs, :] + (ext[5, t, rs, :] - geom[2, t, rs, :] * (ee[t] - ec[t]))
                vn = ext[4, t, rs, :] + (ext[6, t, rs, :] - geom[3, t, rs, :] * (ext[2, t, rn, :] - ec[t]))
                ext[3, t, rs, :] = un
                ext[4, t, rs, :] = vn
                if t < 2 and BASE <= c < BASE + ROWS:
                    cs = pl.ds(c - BASE, chunk)
                    avg[0, t, cs, :] += wn * un
                    avg[1, t, cs, :] += wn * vn
        return carry

    wait_send(force_copies)
    lax.fori_loop(0, NSUB, subcycle, 0)

    for c in range(0, ROWS, chunk):
        hu, hv = face_thickness(c)
        rs, cs = pl.ds(BASE + c, chunk), pl.ds(c, chunk)
        for t in range(2):
            ku, kv = geom[0, t, rs, :], geom[1, t, rs, :]
            geo_ref[0, t, cs, :] = ext[0, t, rs, :]
            geo_ref[1, t, cs, :] = ku
            geo_ref[2, t, cs, :] = kv
            for f, kf, hf in ((0, ku, hu), (1, kv, hv)):
                safe = jnp.where(kf > 0.0, kf * hf[t], 1.0)
                geo_ref[3 + f, t, cs, :] = (avg[f, t, cs, :] * (1.0 / DTB)) / safe - force[f, t, cs, :]
            bt_ref[0, t, cs, :] = ext[2, t, rs, :]
            bt_ref[1, t, cs, :] = ext[3, t, rs, :] * (1.0 / DTB)
            bt_ref[2, t, cs, :] = ext[4, t, rs, :] * (1.0 / DTB)

    for cp in outs:
        cp.wait()
    pred_out.wait()
    wait_send(geo_copies)
    wait_send(ts_copies)
    for g, copies in enumerate(ew_copies):
        if g >= 2:
            wait_recv(copies)
        wait_send(copies)
    wait_recv(tr_copies)
    wait_send(tr_copies)


def tracer_kernel(
    num_row,
    u_hbm, v_hbm, t_hbm, s_hbm, tr_hbm, pred_hbm, geo_ref, bt_ref, hn_hbm, hs_hbm, hts_hbm, ew_ref, uw_ref, vs_hbm,
    eta_out, tu_out, tv_out, un_hbm, vn_hbm, tn_hbm, sn_hbm, trn_hbm,
    qbuf, dbuf, coef,
    isem, hsem, osem,
):
    row = lax.axis_index("row")
    has_s = row > 0
    has_n = row < num_row - 1
    own = pl.ds(8, ROWS)
    npair = 1 + NTR // 2

    def block_reads(p):
        slot = p % 2
        cps = []
        for f in range(2):
            for t in range(2):
                lanes = pl.ds(t * LANES, LANES)
                if p == 0:
                    src = (t_hbm, s_hbm)[f].at[:, :, lanes]
                elif p < npair:
                    src = tr_hbm.at[:, 2 * (p - 1) + f, :, lanes]
                else:
                    src = pred_hbm.at[f, :, t]
                cps.append(pltpu.make_async_copy(src, qbuf.at[slot, f, :, t, own, :], isem.at[slot, f, t]))
        return cps

    def halo_reads(p):
        slot = p % 2
        north, south = [], []
        if p >= npair:
            return north, south
        for f in range(2):
            for t in range(2):
                lanes = pl.ds(t * LANES, LANES)
                if p == 0:
                    sn, ss = hts_hbm.at[0, f, :, t], hts_hbm.at[1, f, :, t]
                else:
                    q = 2 * (p - 1) + f
                    sn, ss = hn_hbm.at[:, q, :, lanes], hs_hbm.at[:, q, :, lanes]
                north.append(pltpu.make_async_copy(sn, qbuf.at[slot, f, :, t, pl.ds(72, 1), :], hsem.at[slot, 0, f, t]))
                south.append(pltpu.make_async_copy(ss, qbuf.at[slot, f, :, t, pl.ds(7, 1), :], hsem.at[slot, 1, f, t]))
        return north, south

    def for_all(p, action):
        for cp in block_reads(p):
            action(cp)
        north, south = halo_reads(p)
        if north:

            @pl.when(has_n)
            def _():
                for cp in north:
                    action(cp)

            @pl.when(has_s)
            def _():
                for cp in south:
                    action(cp)

    def out_copies(p):
        slot = p % 2
        cps = []
        for f in range(2):
            for t in range(2):
                lanes = pl.ds(t * LANES, LANES)
                if p == 0:
                    dst = (tn_hbm, sn_hbm)[f].at[:, :, lanes]
                elif p < npair:
                    dst = trn_hbm.at[:, 2 * (p - 1) + f, :, lanes]
                else:
                    dst = (un_hbm, vn_hbm)[f].at[:, :, lanes]
                cps.append(pltpu.make_async_copy(dbuf.at[slot, f, :, t], dst, osem.at[slot, f, t]))
        return cps

    vel = []
    for f, ref in enumerate((u_hbm, v_hbm)):
        for t in range(2):
            vel.append(
                pltpu.make_async_copy(
                    ref.at[:, :, pl.ds(t * LANES, LANES)], qbuf.at[1, f, :, t, own, :], isem.at[1, f, t]
                )
            )
    for t in range(2):
        vel.append(pltpu.make_async_copy(vs_hbm.at[:, t], qbuf.at[1, 1, :, t, pl.ds(7, 1), :], hsem.at[1, 1, 1, t]))
    for cp in vel:
        cp.start()

    def zero_rows(r):
        def body(k, carry):
            for f in range(2):
                for t in range(2):
                    qbuf[0, f, k, t, pl.ds(r, 1), :] = jnp.zeros((1, LANES), F32)
            return carry

        lax.fori_loop(0, LEV, body, 0)

    @pl.when(jnp.logical_not(has_s))
    def _():
        zero_rows(7)

    @pl.when(jnp.logical_not(has_n))
    def _():
        zero_rows(72)

    for_all(0, lambda cp: cp.start())
    for t in range(2):
        lanes = pl.ds(t * LANES, LANES)
        for i, ref in enumerate((eta_out, tu_out, tv_out)):
            ref[:, lanes] = bt_ref[i, t]
    first_lane, last_lane = lane_iota(8) == 0, lane_iota(8) == LANES - 1
    for cp in vel:
        cp.wait()

    def coef_rows(b, carry):
        r0 = pl.multiple_of(b * 8, 8)
        rs = pl.ds(r0, 8)
        km = [geo_ref[0, t, rs, :] for t in range(2)]
        ku = [geo_ref[1, t, rs, :] for t in range(2)]
        kv = [geo_ref[2, t, rs, :] for t in range(2)]
        for k in range(LEV):
            kf = float(k)
            um = [jnp.where(ku[t] > kf, qbuf[1, 0, k, t, pl.ds(r0 + 8, 8), :], 0.0) for t in range(2)]
            rolled = [pltpu.roll(x, 1, 1) for x in um]
            edge = pltpu.roll(uw_ref[k, rs, :], 1, 1)
            uw = [jnp.where(first_lane, edge, rolled[0]), jnp.where(first_lane, rolled[0], rolled[1])]
            for t in range(2):
                inv = inv_pivot(km[t], k, DIFF_MID, DIFF_LAST)
                dti = DT_STEP * inv
                vm = jnp.where(kv[t] > kf, qbuf[1, 1, k, t, pl.ds(r0 + 8, 8), :], 0.0)
                vs = coef[5, k, t, rs, :]
                ue_in, uw_in = jnp.minimum(um[t], 0.0), jnp.maximum(uw[t], 0.0)
                vn_in, vs_in = jnp.minimum(vm, 0.0), jnp.maximum(vs, 0.0)
                out = (jnp.maximum(um[t], 0.0) - jnp.minimum(uw[t], 0.0)) + (
                    jnp.maximum(vm, 0.0) - jnp.minimum(vs, 0.0)
                )
                coef[0, k, t, rs, :] = inv - dti * out
                coef[1, k, t, rs, :] = -dti * ue_in
                coef[2, k, t, rs, :] = dti * uw_in
                coef[3, k, t, rs, :] = -dti * vn_in
                coef[4, k, t, rs, :] = dti * vs_in
                coef[5, k, t, rs, :] = R_DIFF * inv
        return carry

    def south_level(k, carry):
        kf = k.astype(F32)
        for t in range(2):
            v0 = qbuf[1, 1, k, t, own, :]
            qbuf[1, 1, k, t, own, :] = jnp.where(geo_ref[2, t] > kf, v0, 0.0)
            coef[5, k, t] = qbuf[1, 1, k, t, pl.ds(7, ROWS), :]
        return carry

    lax.fori_loop(0, LEV, south_level, 0)
    lax.fori_loop(0, ROWS // 8, coef_rows, 0)

    def wall_rows_again():
        def body_at(r):
            def body(k, carry):
                for f in range(2):
                    for t in range(2):
                        qbuf[1, f, k, t, pl.ds(r, 1), :] = jnp.zeros((1, LANES), F32)
                return carry

            lax.fori_loop(0, LEV, body, 0)

        @pl.when(jnp.logical_not(has_s))
        def _():
            body_at(7)

        @pl.when(jnp.logical_not(has_n))
        def _():
            body_at(72)

    wall_rows_again()

    for p in range(npair + 1):
        slot = p % 2
        for_all(p, lambda cp: cp.wait())
        if p < npair:
            for_all(p + 1, lambda cp: cp.start())
        if p >= 2:
            for cp in out_copies(p - 2):
                cp.wait()

        if p < npair:

            def pair_rows(b, carry, p=p, slot=slot):
                r0 = pl.multiple_of(b * 8, 8)
                rs = pl.ds(r0, 8)
                ew = ew_ref[p, rs, :]
                prev = [[None, None], [None, None]]
                for k in range(LEV):
                    cf = [[coef[i, k, t, rs, :] for t in range(2)] for i in range(6)]
                    for f in range(2):
                        s = k + f * LEV
                        q = [qbuf[slot, f, k, t, pl.ds(r0 + 8, 8), :] for t in range(2)]
                        qn = [qbuf[slot, f, k, t, pl.ds(r0 + 9, 8), :] for t in range(2)]
                        qs = [qbuf[slot, f, k, t, pl.ds(r0 + 7, 8), :] for t in range(2)]
                        he = pltpu.roll(ew, (2 * LANES - 2 - 2 * s) % LANES, 1)
                        hw = pltpu.roll(ew, (LANES - 2 * s) % LANES, 1) if s else ew
                        re = [pltpu.roll(x, LANES - 1, 1) for x in q]
                        rw = [pltpu.roll(x, 1, 1) for x in q]
                        qe = [jnp.where(last_lane, re[1], re[0]), jnp.where(last_lane, he, re[1])]
                        qw = [jnp.where(first_lane, hw, rw[0]), jnp.where(first_lane, rw[0], rw[1])]
                        for t in range(2):
                            d = (
                                (cf[0][t] * q[t] + cf[1][t] * qe[t])
                                + (cf[2][t] * qw[t] + cf[3][t] * qn[t])
                                + cf[4][t] * qs[t]
                            )
                            if k:
                                d = d + cf[5][t] * prev[f][t]
                            prev[f][t] = d
                            dbuf[slot, f, k, t, rs, :] = d
                for k in range(LEV - 2, -1, -1):
                    for f in range(2):
                        for t in range(2):
                            prev[f][t] = dbuf[slot, f, k, t, rs, :] + (R_DIFF * DIFF_MID[k]) * prev[f][t]
                            dbuf[slot, f, k, t, rs, :] = prev[f][t]
                return carry

            lax.fori_loop(0, ROWS // 8, pair_rows, 0)
        else:

            def correct_level(k, carry, slot=slot):
                kf = k.astype(F32)
                for f in range(2):
                    for t in range(2):
                        dbuf[slot, f, k, t] = jnp.where(
                            geo_ref[1 + f, t] > kf, qbuf[slot, f, k, t, own, :] + geo_ref[3 + f, t], 0.0
                        )
                return carry

            lax.fori_loop(0, LEV, correct_level, 0)
        for cp in out_copies(p):
            cp.start()
    for p in (npair - 1, npair):
        for cp in out_copies(p):
            cp.wait()


def solution(mesh):
    num_col = mesh.shape["col"]
    num_row = mesh.shape["row"]
    hbm = pl.BlockSpec(memory_space=pltpu.HBM)
    vmem = pl.BlockSpec(memory_space=pltpu.VMEM)

    def sds(*shape):
        return jax.ShapeDtypeStruct(shape, F32)

    def local_step(vel_u, vel_v, temperature, salinity, tracers, surf_eta, trans_u, trans_v, bottom, levels, weights):
        wide = 2 * LANES
        mid = pl.pallas_call(
            functools.partial(momentum_kernel, num_col, num_row),
            out_shape=(
                sds(2, LEV, 2, ROWS, LANES),
                sds(5, 2, ROWS, LANES),
                sds(3, 2, ROWS, LANES),
                sds(LEV, NTR, 1, wide),
                sds(LEV, NTR, 1, wide),
                sds(2, 2, LEV, 2, 1, LANES),
                sds(1 + NTR // 2, ROWS, LANES),
                sds(LEV, ROWS, LANES),
                sds(LEV, 2, 1, LANES),
            ),
            in_specs=[hbm] * 10 + [pl.BlockSpec(memory_space=pltpu.SMEM)],
            out_specs=(hbm, vmem, vmem, hbm, hbm, hbm, hbm, hbm, hbm),
            scratch_shapes=[
                pltpu.VMEM((4, LEV, 3, PROWS, LANES), F32),
                pltpu.VMEM((LEV, 3, PROWS, LANES), F32),
                pltpu.VMEM((2, LEV, 2, ROWS, LANES), F32),
                pltpu.VMEM((2, LEV, 2, ROWS, wide), F32),
                pltpu.VMEM((7, 3, EROWS, LANES), F32),
                pltpu.VMEM((7, ROWS, LANES), F32),
                pltpu.VMEM((6, 3, EROWS, LANES), F32),
                pltpu.VMEM((2, ROWS, LANES), jnp.int32),
                pltpu.VMEM((3, PROWS, LANES), F32),
                pltpu.VMEM((2, 2, ROWS, LANES), F32),
                pltpu.VMEM((2, 2, ROWS, LANES), F32),
                pltpu.VMEM((2 + NTR // 2, ROWS, LANES), F32),
                pltpu.VMEM((2, ROWS, LANES), F32),
                pltpu.SemaphoreType.DMA((9, 2)),
                pltpu.SemaphoreType.DMA((2,)),
                pltpu.SemaphoreType.DMA((6,)),
                pltpu.SemaphoreType.DMA((30,)),
                pltpu.SemaphoreType.DMA((30,)),
            ],
            compiler_params=pltpu.CompilerParams(
                collective_id=0, has_side_effects=True, vmem_limit_bytes=56 * 2**20
            ),
            name="momentum",
        )(vel_u, vel_v, temperature, salinity, tracers, surf_eta, trans_u, trans_v, bottom, levels, weights)
        pred, geo, bt, hn, hs, hts, ew, uw, vs = mid
        return pl.pallas_call(
            functools.partial(tracer_kernel, num_row),
            out_shape=(
                sds(ROWS, wide), sds(ROWS, wide), sds(ROWS, wide),
                sds(LEV, ROWS, wide), sds(LEV, ROWS, wide), sds(LEV, ROWS, wide), sds(LEV, ROWS, wide),
                sds(LEV, NTR, ROWS, wide),
            ),
            in_specs=[hbm] * 6 + [vmem, vmem, hbm, hbm, hbm, vmem, vmem, hbm],
            out_specs=(vmem,) * 3 + (hbm,) * 5,
            scratch_shapes=[
                pltpu.VMEM((2, 2, LEV, 2, PROWS, LANES), F32),
                pltpu.VMEM((2, 2, LEV, 2, ROWS, LANES), F32),
                pltpu.VMEM((6, LEV, 2, ROWS, LANES), F32),
                pltpu.SemaphoreType.DMA((2, 2, 2)),
                pltpu.SemaphoreType.DMA((2, 2, 2, 2)),
                pltpu.SemaphoreType.DMA((2, 2, 2)),
            ],
            compiler_params=pltpu.CompilerParams(vmem_limit_bytes=56 * 2**20),
            name="tracers",
        )(vel_u, vel_v, temperature, salinity, tracers, pred, geo, bt, hn, hs, hts, ew, uw, vs)

    spec_3d = P(None, "row", "col")
    spec_4d = P(None, None, "row", "col")
    spec_2d = P("row", "col")
    in_specs = (spec_3d, spec_3d, spec_3d, spec_3d, spec_4d, spec_2d, spec_2d, spec_2d, spec_2d, spec_2d, P())
    out_specs = (spec_2d, spec_2d, spec_2d, spec_3d, spec_3d, spec_3d, spec_3d, spec_4d)
    return jax.shard_map(local_step, mesh=mesh, in_specs=in_specs, out_specs=out_specs, check_vma=False)
```

time: 1950 us -> 108 us (0.06); the launches traced: 1920 us -> 107 us
  other arithmetic: 916 us -> 0 us
  local copies, waits for them, and re-layouts: 549 us -> 0 us
  starting transfers between devices: 336 us -> 0 us
  waiting for transfers between devices: 110 us -> 0 us
  Pallas kernels: 0 us -> 106 us
    dynamic_update_slice x403 -> x0, other arithmetic: 590 us -> none  [the longest x310 444 us: tridiag_apply(): lax.scan(fwd_step, jnp.zeros_like(rhs_all[0]), (sub_diag, pivots, rhs_all))]
    ppermute x148 -> x0, starting transfers between devices: 336 us -> none  [the longest x36 179 us: shift_south(): edge_strip = lax.ppermute(grid_field[..., -1:, :], 'row', to_north)]
    mul x40 -> x0, other arithmetic: 232 us -> none  [the longest x1 92.6 us: local_step(): advect_tracer(tracers, u_face[:, None], v_face[:, None]) * mask_t]
    slice x230 -> x0, local copies, waits for them, and re-layouts: 207 us -> none  [the longest x34 57.6 us: shift_south(): edge_strip = lax.ppermute(grid_field[..., -1:, :], 'row', to_north)]
    unnamed x138 -> x0, local copies, waits for them, and re-layouts: 113 us -> none
    ppermute x148 -> x0, waiting for transfers between devices: 110 us -> none  [the longest x35 48.7 us: shift_west(): edge_strip = lax.ppermute(grid_field[..., -1:], 'col', to_east)]
    pallas_call x0 -> x2, Pallas kernels: none -> 106 us  [the longest x1 63.4 us: local_step(): pl.pallas_call(functools.partial(momentum_kernel, num_col, num_row), out_...]
    ppermute x11 -> x0, local copies, waits for them, and re-layouts: 58.7 us -> none  [the longest x1 20.8 us: shift_north(): edge_strip = lax.ppermute(grid_field[..., :1, :], 'row', to_south)]
  transfers between devices with their start and end apart: 148 -> 0, of which waited for: 90 -> 0; matrix products, arithmetic and copies ran while one was open for 46% -> 0% of each run, Pallas kernels for 0% -> 0%
where the time goes in v1:
time: 108 us; the launch traced here: 107 us
  Pallas kernels  106 us (98%)
    pallas_call x1, Pallas kernels, local_step(): pl.pallas_call(functools.partial(momentum_kernel, num_col, num_row), out_...  63.4 us
    pallas_call x1, Pallas kernels, local_step(): pl.pallas_call(functools.partial(tracer_kernel, num_row), out_shape=(sds(...  42.5 us

profile of v1, /device:TPU:3, one launch (start us, length us, event | category | flops | bytes accessed | tf_op | source)
XLA Modules:
  0.0 106.5 jit_solution(4225844973521394000)
XLA Ops:
  0.6 63.4 %momentum.1 = (f32[2,31,2,64,128]{4,3,2,1,0:T(8,128)}, f32[5,2,64,128]{3,2,1,0:T(8,128)}, f32[3,2,64,128]{3,2,1,0:T(8,128)}, f32[31,10,1,256]{3,2,1,0:T(1,128)},...) custom-call(f32[31,64,256]{2,1,0:T(8,128)} %u_hbm.3, ...), custom_call_target="tpu_custom_call" | custom-call | tf_op jit(solution)/shard_map/momentum/pallas_call | solution.py:734
  64.0 42.5 %tracers.1 = (f32[64,256]{1,0:T(8,128)}, f32[64,256]{1,0:T(8,128)}, f32[64,256]{1,0:T(8,128)}, f32[31,64,256]{2,1,0:T(8,128)}, f32[31,64,256]{2,1,0:T(8,128)}, /...) custom-call(f32[31,64,256]{2,1,0:T(8,128)} %u_hbm.3, f32[31,64,256]{2,1,0:T(8,128)} %v_hbm.3, ...), custom_call_target="tpu_custom_call" | custom-call | tf_op jit(solution)/shard_map/tracers/pallas_call | solution.py:775
